TPU v7x, 512 devices: a 4x2x32 block of a 4x8x32 slice. The times are simulated.
512 devices in a mesh: grp: 2 (over y), seq: 32 (over z), head: 4 (over x), batch: 2 (over core).
Axes of the slice: x: 4, y: 2, z: 32, core: 2. Of those that a mesh axis runs over, the one named last changes fastest.
The devices are a block of a 4x8x32 slice.
Arguments:
- queries: bfloat16 [64, 64, 128], P(('grp', 'batch'), 'head'), parts along dimension 0, may hold values from -8 to 8
- key_cache: bfloat16 [64, 8, 8192, 128], P(('grp', 'batch'), 'head', 'seq'), parts along dimension 0, may hold values from -5 to 5
- value_cache: bfloat16 [64, 8, 8192, 128], P(('grp', 'batch'), 'head', 'seq'), parts along dimension 0, may hold values from -5 to 5
- gate_logits: float32 [2, 64, 64], P(None, ('grp', 'batch'), 'head'), parts along dimension 1, may hold values from -6 to 6
- lengths: int32 [64], P(('grp', 'batch')), parts along dimension 0, may hold values from 2048 to 8192, as said below
- chosen: int32 [64, 8, 16], P(('grp', 'batch'), 'head'), parts along dimension 0, may hold values from 0 to 63, as said below
- counts: int32 [64, 8], P(('grp', 'batch'), 'head'), parts along dimension 0, may hold values from 1 to 16, as said below
Outputs:
- output: bfloat16 [64, 64, 128], P(('grp', 'batch'), 'head'), parts along dimension 0
There are 2 independent parts, one for each index of `grp`. A program takes and returns all parts, laid end to end along the dimension named above; each array names one. Nothing has to cross between parts.
Inputs may be any that keep to these rules, and one draw needn't show every extreme that they name: `lengths`: every draw has a sequence of the full length 8192. `chosen`: for each sequence and key-value head the first counts entries are distinct blocks that start below the sequence's length, and the first entry is block 0; the entries after them are ignored. `counts`: every draw has a sequence with 16 valid entries for every key-value head.
All inputs are finite; a program needn't handle non-finite values.
Results may differ from a plain program's by a relative error of at most 0.02.
Values may be sent and summed in bfloat16 or wider, within the bound.
A program may use at most 64 MiB of HBM per device.

v0:
```python
import math

import jax
import jax.numpy as jnp
from jax import lax
from jax.sharding import PartitionSpec as P

BLOCK = 128


def collected_together(array, axis):
    leaves = jax.tree.leaves(array)
    sequence = sorted(range(len(leaves)), key=lambda k: -leaves[k].size)
    width = (1, *leaves[sequence[0]].shape)[-1]
    lines = [
        jnp.pad(leaves[k].reshape(-1), (0, -leaves[k].size % width)).reshape(-1, width)
        for k in sequence
    ]
    both, at, found = (lax.all_gather(jnp.concatenate(lines), axis), 0, {})
    for k, line in zip(sequence, lines):
        piece = both[:, at : at + len(line)].reshape(len(both), -1)
        found[k] = piece[:, : leaves[k].size].reshape(-1, *leaves[k].shape)
        at += len(line)
    numbers = iter(range(len(leaves)))
    return jax.tree.map(lambda _: found[next(numbers)], array)


def combined_all(array, axis, join):
    gathered = collected_together(
        jax.tree.map(
            lambda a, kind: a.astype(kind), array, (jnp.bfloat16, jnp.bfloat16, jnp.bfloat16)
        ),
        axis,
    )

    def take(source):
        return jax.tree.map(
            lambda a, own: lax.dynamic_index_in_dim(a, source, 0, False).astype(own.dtype),
            gathered,
            array,
        )

    return lax.fori_loop(
        1, lax.axis_size(axis), lambda source, state: join(state, take(source)), take(0)
    )


def softmax_terms(query_rows, key_rows, value_rows, live_mask, score_scale):
    scores = (
        jnp.einsum("pgd,pnd->pgn", query_rows, key_rows, preferred_element_type=jnp.float32)
        * score_scale
    )
    scores = jnp.where(live_mask[:, None, :], scores, -1e30)
    row_max = jnp.max(scores, axis=2)
    weights = jnp.where(live_mask[:, None, :], jnp.exp(scores - row_max[:, :, None]), 0.0)
    weight_sum = jnp.sum(weights, axis=2)
    summed = jnp.einsum(
        "pgn,pnd->pgd", weights.astype(jnp.bfloat16), value_rows, preferred_element_type=jnp.float32
    )
    return (row_max, weight_sum, summed)


def combine(first, second):
    merged = []
    for index in range(0, len(first), 3):
        row_max = jnp.maximum(first[index], second[index])
        factor_first = jnp.exp(first[index] - row_max)
        factor_second = jnp.exp(second[index] - row_max)
        merged.append(row_max)
        merged.append(first[index + 1] * factor_first + second[index + 1] * factor_second)
        merged.append(
            first[index + 2] * factor_first[:, :, None]
            + second[index + 2] * factor_second[:, :, None]
        )
    return tuple(merged)


def finish(weight_sum, summed):
    return summed / weight_sum[:, :, None]


def pool_blocks(key_rows, value_rows, pair_lengths, first_block):
    pair_count, tokens, head_width = key_rows.shape
    block_count = tokens // BLOCK
    position = first_block * BLOCK + jnp.arange(tokens, dtype=jnp.int32)
    live_mask = position[None, :] < pair_lengths[:, None]
    token_ones = live_mask.astype(jnp.bfloat16).reshape(pair_count, block_count, BLOCK)
    starts = (first_block + jnp.arange(block_count, dtype=jnp.int32)) * BLOCK
    filled = jnp.clip(pair_lengths[:, None] - starts[None, :], 0, BLOCK)
    root_fill = jnp.sqrt(jnp.maximum(filled, 1).astype(jnp.float32))[:, :, None]
    key_sums = jnp.einsum(
        "pjt,pjtd->pjd",
        token_ones,
        key_rows.reshape(pair_count, block_count, BLOCK, head_width),
        preferred_element_type=jnp.float32,
    )
    value_sums = jnp.einsum(
        "pjt,pjtd->pjd",
        token_ones,
        value_rows.reshape(pair_count, block_count, BLOCK, head_width),
        preferred_element_type=jnp.float32,
    )
    pooled_keys = (key_sums / root_fill).astype(jnp.bfloat16)
    pooled_values = (value_sums / root_fill).astype(jnp.bfloat16)
    return (live_mask, filled > 0, pooled_keys, pooled_values)


def picked_tokens(live_mask, chosen_rows, count_rows, first_block):
    pair_count, tokens = live_mask.shape
    block_count = tokens // BLOCK
    block_ids = first_block + jnp.arange(block_count, dtype=jnp.int32)
    slot_live = jnp.arange(chosen_rows.shape[1], dtype=jnp.int32)[None, :] < count_rows[:, None]
    picked = jnp.any(
        (chosen_rows[:, :, None] == block_ids[None, None, :]) & slot_live[:, :, None], axis=1
    )
    spread = jnp.broadcast_to(picked[:, :, None], (pair_count, block_count, BLOCK)).reshape(
        pair_count, tokens
    )
    return live_mask & spread


def blend_gates(compressed, selected, gate_pairs):
    mixed = gate_pairs[0][:, :, None] * compressed + gate_pairs[1][:, :, None] * selected
    return mixed.astype(jnp.bfloat16)


def on_device(queries, key_cache, value_cache, gate_logits, lengths, chosen, counts):
    batch_rows, head_count, context, head_width = key_cache.shape
    pair_count = batch_rows * head_count
    group_size = queries.shape[1] // head_count
    score_scale = 1.0 / math.sqrt(head_width)
    query_rows = queries.reshape(pair_count, group_size, head_width)
    pair_keys = key_cache.reshape(pair_count, context, head_width)
    pair_values = value_cache.reshape(pair_count, context, head_width)
    pair_lengths = jnp.broadcast_to(lengths[:, None], (batch_rows, head_count)).reshape(pair_count)
    pair_chosen = chosen.reshape(pair_count, chosen.shape[2])
    pair_counts = counts.reshape(pair_count)
    gate_pairs = jax.nn.sigmoid(gate_logits.reshape(2, pair_count, group_size))
    local_blocks = context // BLOCK
    first_block = lax.axis_index("seq") * local_blocks
    live_mask, block_live, pooled_keys, pooled_values = pool_blocks(
        pair_keys, pair_values, pair_lengths, first_block
    )
    token_mask = picked_tokens(live_mask, pair_chosen, pair_counts, first_block)
    all_keys, all_values = (
        lax.all_gather(pooled_keys, "seq", axis=1, tiled=True),
        lax.all_gather(pooled_values, "seq", axis=1, tiled=True),
    )
    all_starts = jnp.arange(all_keys.shape[1], dtype=jnp.int32) * BLOCK
    all_live = all_starts[None, :] < pair_lengths[:, None]
    s_max, s_sum, s_val = softmax_terms(query_rows, pair_keys, pair_values, token_mask, score_scale)
    merged = combined_all((s_max, s_sum, s_val), "seq", combine)
    c_max, c_sum, c_val = softmax_terms(query_rows, all_keys, all_values, all_live, score_scale)
    output = blend_gates(finish(c_sum, c_val), finish(merged[1], merged[2]), gate_pairs)
    return output.reshape(batch_rows, head_count * group_size, head_width)


def solution(mesh):
    return jax.shard_map(
        on_device,
        mesh=mesh,
        in_specs=(
            P(("grp", "batch"), "head", None),
            P(("grp", "batch"), "head", "seq", None),
            P(("grp", "batch"), "head", "seq", None),
            P(None, ("grp", "batch"), "head"),
            P(("grp", "batch")),
            P(("grp", "batch"), "head", None),
            P(("grp", "batch"), "head"),
        ),
        out_specs=P(("grp", "batch"), "head", None),
        check_vma=False,
    )
```

profile of v0, /device:TPU:40, one launch (start us, length us, event | category | flops | bytes accessed | tf_op | source)
XLA Modules:
  0.0 226.3 jit_solution(120527223969621659)
XLA Ops:
  6.6 0.9 broadcast_in_dim.71
  7.4 0.1 lt.87
  7.5 0.8 copy.48
  8.3 0.1 lt.97
  8.4 0.8 copy.47
  9.2 0.1 and_reduce_fusion
  9.3 0.1 copy.49
  9.4 0.1 broadcast_in_dim.76
  9.6 1.7 fusion.34
  11.3 0.2 fusion.16
  11.5 0.4 fusion.13
  11.9 0.1 convert_element_type.106
  12.0 0.1 convert_element_type.104
  12.1 0.6 maximum_bitcast_fusion
  13.2 0.1 compare_bitcast_fusion
  13.3 2.3 %fusion.22 = f32[32,2,1,128]{3,2,1,0:T(1,128)S(1)} fusion(bf16[32,2,128,128]{3,2,1,0:T(8,128)(2,1)} %bitcast.62, pred[32,2,128,1]{2,1,0,3:T(4,128)(4,1)S(1)} %compare_bitcast_fusion), kind=kOutput, calls=%fused_computation.32 | convolution fusion | flops 2097152 | bytes 2138112 | tf_op jit(solution)/shard_map/pjt,pjtd->pjd/dot_general | solution.py:97
  15.6 0.7 fusion.24
  16.2 0.1 fusion.29
  16.3 98.8 %all_gather.12 = bf16[32,64,128]{2,0,1:T(8,128)(2,1)S(1)} all-gather(bf16[32,2,128]{2,0,1:T(8,128)(2,1)S(1)} %get-tuple-element.236), channel_id=1, replica_groups=mesh['grp'=2,'seq'=32,'head'=4,'batch'=2] {'seq'}, dimensions={1}, use_global_device_ids=true | all-gather | bytes 540672 | tf_op jit(solution)/shard_map/all_gather | solution.py:146
  115.1 0.6 fusion.35
  115.7 55.1 %all_gather.13 = bf16[32,64,128]{2,0,1:T(8,128)(2,1)S(1)} all-gather(bf16[32,2,128]{2,0,1:T(8,128)(2,1)S(1)} %get-tuple-element.237), channel_id=1, replica_groups=mesh['grp'=2,'seq'=32,'head'=4,'batch'=2] {'seq'}, dimensions={1}, use_global_device_ids=true | all-gather | bytes 540672 | tf_op jit(solution)/shard_map/all_gather | solution.py:147
  170.7 4.0 %all-gather.4.cloned.1.call-done = bf16[32,260,128]{2,1,0:T(8,128)(2,1)} async-done(((bf16[1,260,128]{2,1,0:T(8,128)(2,1)}), bf16[32,260,128]{2,1,0:T(8,128)(2,1)}) %all-gather.4.cloned.1.call-update) | async-done | bytes 2129936 | tf_op jit(solution)/shard_map/all_gather | solution.py:19
  174.7 0.9 fusion.32
  175.6 0.1 copy.60
  175.8 0.1 copy.54
  175.9 0.1 copy.61
  176.0 0.1 copy.55
  176.2 0.8 slice_convert_fusion
  177.2 0.1 copy.53
  177.2 3.1 %slice_bitcast_fusion = bf16[32,32,8,128]{3,2,1,0:T(8,128)(2,1)} fusion(bf16[32,260,128]{2,1,0:T(8,128)(2,1)} %all-gather.4.cloned.1.call-done), kind=kLoop, calls=%fused_computation.9 | loop fusion | bytes 4194304 | tf_op jit(solution)/shard_map/reshape;reshape | solution.py:22
  180.4 0.8 fusion.26
  181.2 37.2 %while.19 = (s32[]{:T(128)}, f32[32,8]{0,1:T(8,128)S(1)}, f32[32,8]{0,1:T(8,128)S(1)}, f32[32,8,128]{2,1,0:T(8,128)S(1)}, bf16[32,32,8]{1,2,0:T(8,128)(2,1)S(1)}...) while((s32[]{:T(128)}, f32[32,8]{0,1:T(8,128)S(1)}, ...), condition=%wide.region_6.7_spmd, body=%wide.region_5.6_spmd.sunk | while | flops 133125 | bytes 341143 | solution.py:43
  181.4 1.0 fusion.48
  182.6 1.0 fusion.48
  183.8 1.0 fusion.48
  185.0 1.0 fusion.48
  186.2 1.0 fusion.48
  187.4 1.0 fusion.48
  188.6 1.0 fusion.48
  189.8 1.0 fusion.48
  191.0 1.0 fusion.48
  192.2 1.0 fusion.48
  193.4 1.0 fusion.48
  194.6 1.0 fusion.48
  195.8 1.0 fusion.48
  197.0 1.0 fusion.48
  198.2 1.0 fusion.48
  199.4 1.0 fusion.48
  200.6 1.0 fusion.48
  201.8 1.0 fusion.48
  203.0 1.0 fusion.48
  204.2 1.0 fusion.48
  205.4 1.0 fusion.48
  206.6 1.0 fusion.48
  207.8 1.0 fusion.48
  209.0 1.0 fusion.48
  210.2 1.0 fusion.48
  211.4 1.0 fusion.48
  212.6 1.0 fusion.48
  213.8 1.0 fusion.48
  215.0 1.0 fusion.48
  216.3 1.0 fusion.48
  217.5 1.0 fusion.48
  218.5 0.9 fusion.12
  (120 shorter events, 6.0 us)
Async XLA Ops:
  6.5 3.0 %copy-start = (bf16[16,2,256,128]{3,2,1,0:T(8,128)(2,1)S(1)}, bf16[16,2,256,128]{3,2,1,0:T(8,128)(2,1)}, u32[]{:S(2)}) copy-start(bf16[16,2,256,128]{3,2,1,0:T(8,128)(2,1)} %param.10) | copy-start | bytes 6291460
  6.6 168.1 %all-gather.4.cloned.1.call-start = ((), (), s32[]{:S(2)}) async-start(), calls=%async_computation | async-start | bytes 2230272 | tf_op jit(solution)/shard_map/all_gather | solution.py:19
  9.4 2.1 copy-start.1
  11.3 1.6 copy-start.3
  13.3 101.8 %copy-start.2 = (bf16[16,16,128]{2,1,0:T(8,128)(2,1)S(1)}, bf16[16,16,128]{2,1,0:T(8,128)(2,1)}, u32[]{:S(2)}) copy-start(bf16[16,16,128]{2,1,0:T(8,128)(2,1)} %param.9) | copy-start | bytes 196612
Sparse Core Ops, SparseCore 0:
  13.0 161.6 all-gather.3
where the time goes:
time: 229 us; the launch traced here: 226 us
  blocking collectives  154 us (67%)
  other arithmetic  34.5 us (15%)
  between operations  13.6 us (6%)
  local copies, waits for them, and re-layouts  12.8 us (6%)
  matrix products  6.53 us (3%)
  waiting for transfers between devices  4.02 us (2%)
    all_gather x1, blocking collectives, on_device(): lax.all_gather(pooled_keys, 'seq', axis=1, tiled=True)  98.8 us
    all_gather x1, blocking collectives, on_device(): lax.all_gather(pooled_values, 'seq', axis=1, tiled=True)  55.1 us
    add x31, other arithmetic, combine(): first[index + 2] * factor_first[:, :, None]  31 us
  transfers between devices with their start and end apart: 1, of which 1 were waited for; matrix products, arithmetic and copies ran while one was open for 2% of the time, Pallas kernels for 0%

commit v1 on v0

v1 whole, which is shorter than its diff:
```python
import functools
import math

import jax
import jax.numpy as jnp
from jax import lax
from jax.experimental import pallas as pl
from jax.experimental.pallas import tpu as pltpu
from jax.sharding import PartitionSpec as P

BLOCK = 128
STRIDE = 4
NEAR = (-1, 1, 2)
CHUNK = 4
PIECE = 32
NEG = -1e30
MESH = pl.DeviceIdType.MESH


def iota(shape, dim):
    return lax.broadcasted_iota(jnp.int32, shape, dim)


def split_logs(logs):
    lane = iota(logs.shape, 1)
    spread = jnp.where(
        lane < PIECE,
        logs,
        jnp.where(lane < 2 * PIECE, pltpu.roll(logs, PIECE, 1), pltpu.roll(logs, 2 * PIECE, 1)),
    )
    high = spread.astype(jnp.bfloat16).astype(jnp.float32)
    rest = spread - high
    middle = rest.astype(jnp.bfloat16).astype(jnp.float32)
    low = rest - middle
    return jnp.where(lane < PIECE, high, jnp.where(lane < 2 * PIECE, middle, low)).astype(jnp.bfloat16)


def join_logs(pieces):
    pieces = pieces.astype(jnp.float32)
    width = pieces.shape[1]
    return (pieces + pltpu.roll(pieces, width - PIECE, 1)) + pltpu.roll(pieces, width - 2 * PIECE, 1)


def column(tile, lane):
    return jnp.broadcast_to(tile[:, lane : lane + 1], tile.shape)


def kernel(
    n,
    q_ref,
    k_hbm,
    v_hbm,
    gate_ref,
    length_ref,
    chosen_ref,
    count_ref,
    out_ref,
    k_buf,
    v_buf,
    sent,
    landed,
    board,
    gate_pad,
    gates,
    k_sem,
    v_sem,
    a_send,
    a_recv,
    b_send,
    b_recv,
):
    me = lax.axis_index("seq")
    sign = 1 - 2 * lax.axis_index("batch")
    rows, heads, context, width = k_buf.shape
    group = q_ref.shape[1] // heads
    local = context // BLOCK
    window = rows
    half = window // 2
    sources = n // window
    tile = heads * group
    scale = 1.0 / math.sqrt(width)

    def at(offset):
        return lax.rem(me + sign * offset + 2 * n, n)

    def remote(src, dst, send, recv, target):
        return pltpu.make_async_remote_copy(
            src_ref=src,
            dst_ref=dst,
            send_sem=send,
            recv_sem=recv,
            device_id={"seq": target},
            device_id_type=MESH,
        )

    barrier = pltpu.get_barrier_semaphore()
    for distance in range(half, 0, -1):
        for offset in (-distance, distance):
            pl.semaphore_signal(barrier, inc=1, device_id={"seq": at(offset)}, device_id_type=MESH)

    def loads(c):
        part = pl.ds(c * CHUNK, CHUNK)
        return (
            pltpu.make_async_copy(k_hbm.at[part], k_buf.at[part], k_sem.at[c]),
            pltpu.make_async_copy(v_hbm.at[part], v_buf.at[part], v_sem.at[c]),
        )

    for c in range(rows // CHUNK):
        for copy in loads(c):
            copy.start()

    gate_pad[...] = jnp.zeros_like(gate_pad)
    for branch in range(2):
        logits = gate_ref[branch]
        gate_pad[branch * rows : (branch + 1) * rows, : heads * group] = 1.0 / (1.0 + jnp.exp(-logits))
    turned = gate_pad[...].T
    lane = iota((group, width), 1)
    for b in range(rows):
        packed = jnp.zeros((group, width), jnp.float32)
        for branch in range(2):
            for h in range(heads):
                c = branch * heads + h
                here = turned[h * group : (h + 1) * group]
                moved = pltpu.roll(here, (c - (1 - branch) * rows - b) % width, 1)
                packed = jnp.where(lane == c, moved, packed)
        gates[b] = packed

    slot = iota((1, chosen_ref.shape[2]), 1)
    first = me * local

    def one_pair(b, h, live, root):
        scores = lax.dot_general(
            q_ref[b], k_buf[b, h], (((1,), (1,)), ((), ())), preferred_element_type=jnp.float32
        )[h * group : (h + 1) * group] * scale
        parts = [scores[:, j * BLOCK : (j + 1) * BLOCK] for j in range(local)]
        chosen = chosen_ref[b, h : h + 1, :]
        listed = slot < count_ref[h, b]
        masks = []
        for j in range(local):
            hit = jnp.where((chosen == first + j) & listed, 1.0, 0.0)
            picked = jnp.max(hit, axis=1, keepdims=True)
            masks.append(live[j] & (jnp.broadcast_to(picked, (group, BLOCK)) > 0.5))
        kept = [jnp.where(m, s, NEG) for m, s in zip(masks, parts)]
        top = jnp.max(functools.reduce(jnp.maximum, kept), axis=1, keepdims=True)
        weights = [jnp.where(m, jnp.exp(s - top), 0.0) for m, s in zip(masks, kept)]
        total = jnp.sum(sum(weights), axis=1, keepdims=True)
        pooled = [
            jnp.where(
                live[j][:, :1],
                jnp.sum(jnp.where(live[j], parts[j], 0.0), axis=1, keepdims=True) * root[j],
                NEG,
            )
            for j in range(local)
        ]
        pool_top = functools.reduce(jnp.maximum, pooled)
        pool_weights = [jnp.where(live[j][:, :1], jnp.exp(pooled[j] - pool_top), 0.0) for j in range(local)]
        pool_total = sum(pool_weights)
        spread = [jnp.where(live[j], pool_weights[j] * root[j], 0.0) for j in range(local)]
        left = jnp.concatenate(
            [jnp.concatenate(weights, axis=1), jnp.concatenate(spread, axis=1)], axis=0
        ).astype(jnp.bfloat16)
        summed = jnp.dot(left, v_buf[b, h], preferred_element_type=jnp.float32)
        result = []
        for top_of, total_of, value in (
            (top, total, summed[:group]),
            (pool_top, pool_total, summed[group:]),
        ):
            some = total_of > 0.0
            safe = jnp.where(some, total_of, 1.0)
            result.append((value / safe, jnp.where(some, top_of + jnp.log(safe), NEG)))
        return result

    def one_row(b):
        length = length_ref[b]
        live, root = [], []
        for j in range(local):
            start = (first + j) * BLOCK
            live.append(start + iota((group, BLOCK), 1) < length)
            filled = jnp.clip(length - start, 1, BLOCK).astype(jnp.float32)
            root.append(1.0 / jnp.sqrt(jnp.full((group, 1), filled, jnp.float32)))
        pairs = [one_pair(b, h, live, root) for h in range(heads)]
        logs = jnp.zeros((group, width), jnp.float32)
        for branch in range(2):
            values = jnp.concatenate([pairs[h][branch][0] for h in range(heads)], axis=0)
            sent[b, branch * tile : (branch + 1) * tile] = values.astype(jnp.bfloat16)
            for h in range(heads):
                logs = jnp.where(lane == branch * heads + h, pairs[h][branch][1], logs)
        sent[b, 2 * tile :] = split_logs(logs)

    def one_chunk(c, carry):
        for copy in loads(c):
            copy.wait()
        for i in range(CHUNK):
            one_row(c * CHUNK + i)
        return carry

    lax.fori_loop(0, rows // CHUNK, one_chunk, 0)

    pl.semaphore_wait(barrier, 2 * half)
    offsets = [d for d in range(-half, half) if d != 0]
    first_copies = []
    for i, offset in enumerate(sorted(offsets, key=lambda d: -abs(d))):
        target = at(offset)
        copy = remote(
            sent.at[lax.rem(target, window)],
            landed.at[offset + half],
            a_send.at[i],
            a_recv.at[offset + half],
            target,
        )
        copy.start()
        first_copies.append(copy)
    for copy in first_copies:
        copy.wait_recv()

    mine = lax.rem(me, window)
    logs = [
        join_logs(sent[mine, 2 * tile :] if d == 0 else landed[d + half, 2 * tile :])
        for d in range(-half, half)
    ]
    top = functools.reduce(jnp.maximum, logs)
    shares = [jnp.exp(x - top) for x in logs]
    total = functools.reduce(jnp.add, shares)
    merged = [jnp.zeros((group, width), jnp.float32) for _ in range(2 * heads)]
    inverse = 1.0 / total
    for share, d in zip(shares, range(-half, half)):
        share = share * inverse
        for c in range(0, 2 * heads, heads):
            part = pl.ds(c * group, tile)
            values = (sent[mine, part] if d == 0 else landed[d + half, part]).astype(jnp.float32)
            for h in range(heads):
                merged[c + h] += column(share, c + h) * values[h * group : (h + 1) * group]
    for branch in range(2):
        board[me, branch * tile : (branch + 1) * tile] = jnp.concatenate(
            merged[branch * heads : (branch + 1) * heads], axis=0
        ).astype(jnp.bfloat16)
    board[me, 2 * tile :] = split_logs(jnp.where(lane < 2 * heads, top + jnp.log(total), 0.0))

    def broadcast(owner, offset, number):
        return remote(board.at[owner], board.at[owner], b_send.at[number], b_recv.at[owner], at(offset))

    steps = []
    for distance in range(STRIDE, n // 2, STRIDE):
        steps += [distance, -distance]
    steps.append(n // 2)
    second_copies = []

    def start(owner, offset):
        copy = broadcast(owner, offset, len(second_copies))
        copy.start()
        second_copies.append(copy)

    for offset in reversed(steps):
        start(me, offset)
    for near in NEAR:
        start(me, near)
    for offset in steps:
        owner = at(-offset)
        broadcast(owner, offset, 0).wait_recv()
        for near in NEAR:
            start(owner, near)
    for offset in [0] + steps:
        for near in NEAR:
            broadcast(at(-offset - near), near, 0).wait_recv()

    for b in range(rows):
        logs = [join_logs(board[s * window + b, 2 * tile :]) for s in range(sources)]
        top = functools.reduce(jnp.maximum, logs)
        shares = [jnp.exp(x - top) for x in logs]
        factor = gates[b] / functools.reduce(jnp.add, shares)
        mixed = [jnp.zeros((group, width), jnp.float32) for _ in range(heads)]
        for s, share in enumerate(shares):
            share = share * factor
            for branch in range(2):
                values = board[s * window + b, branch * tile : (branch + 1) * tile].astype(jnp.float32)
                for h in range(heads):
                    mixed[h] += column(share, branch * heads + h) * values[h * group : (h + 1) * group]
        out_ref[b] = jnp.concatenate(mixed, axis=0).astype(jnp.bfloat16)

    for copy in first_copies + second_copies:
        copy.wait_send()


def on_device(n, queries, key_cache, value_cache, gate_logits, lengths, chosen, counts):
    rows, heads, context, width = key_cache.shape
    group = queries.shape[1] // heads
    window = rows
    lines = 2 * heads * group + group
    relays = len(range(STRIDE, n // 2, STRIDE)) * 2 + 1
    vmem = pl.BlockSpec(memory_space=pltpu.VMEM)
    smem = pl.BlockSpec(memory_space=pltpu.SMEM)
    anywhere = pl.BlockSpec(memory_space=pl.ANY)
    return pl.pallas_call(
        functools.partial(kernel, n),
        name="decode",
        out_shape=jax.ShapeDtypeStruct(queries.shape, jnp.bfloat16),
        in_specs=[vmem, anywhere, anywhere, vmem, smem, vmem, smem],
        out_specs=vmem,
        scratch_shapes=[
            pltpu.VMEM(key_cache.shape, jnp.bfloat16),
            pltpu.VMEM(value_cache.shape, jnp.bfloat16),
            pltpu.VMEM((rows, lines, width), jnp.bfloat16),
            pltpu.VMEM((window, lines, width), jnp.bfloat16),
            pltpu.VMEM((n, lines, width), jnp.bfloat16),
            pltpu.VMEM((width, width), jnp.float32),
            pltpu.VMEM((rows, group, width), jnp.float32),
            pltpu.SemaphoreType.DMA((rows // CHUNK,)),
            pltpu.SemaphoreType.DMA((rows // CHUNK,)),
            pltpu.SemaphoreType.DMA((window,)),
            pltpu.SemaphoreType.DMA((window,)),
            pltpu.SemaphoreType.DMA((relays + len(NEAR) * (relays + 1),)),
            pltpu.SemaphoreType.DMA((n,)),
        ],
        compiler_params=pltpu.CompilerParams(collective_id=0, has_side_effects=True),
    )(queries, key_cache, value_cache, gate_logits, lengths, chosen, counts.T)


def solution(mesh):
    return jax.shard_map(
        functools.partial(on_device, mesh.shape["seq"]),
        mesh=mesh,
        in_specs=(
            P(("grp", "batch"), "head", None),
            P(("grp", "batch"), "head", "seq", None),
            P(("grp", "batch"), "head", "seq", None),
            P(None, ("grp", "batch"), "head"),
            P(("grp", "batch")),
            P(("grp", "batch"), "head", None),
            P(("grp", "batch"), "head"),
        ),
        out_specs=P(("grp", "batch"), "head", None),
        check_vma=False,
    )
```

time: 229 us -> 83.8 us (0.37); the launches traced: 226 us -> 83.6 us
  blocking collectives: 154 us -> 0 us
  Pallas kernels: 0 us -> 82.1 us
  other arithmetic: 34.5 us -> 0 us
  between operations: 13.6 us -> 0.01 us
  local copies, waits for them, and re-layouts: 12.8 us -> 1.47 us
  matrix products: 6.53 us -> 0 us
  waiting for transfers between devices: 4.02 us -> 0 us
    all_gather x2 -> x0, blocking collectives: 154 us -> none  [the longest x1 98.8 us: on_device(): lax.all_gather(pooled_keys, 'seq', axis=1, tiled=True)]
    pallas_call x0 -> x1, Pallas kernels: none -> 82.1 us  [on_device(): pl.pallas_call(functools.partial(kernel, n), name='decode', out_shape=jax...]
    add x65 -> x0, other arithmetic: 31.5 us -> none  [the longest x31 31 us: combine(): first[index + 2] * factor_first[:, :, None]]
    dot_general x5 -> x0, matrix products: 5.98 us -> none  [the longest x1 2.26 us: pool_blocks(): jnp.einsum('pjt,pjtd->pjd', token_ones, value_rows.reshape(pair_count, bl...]
    exp x62 -> x0, local copies, waits for them, and re-layouts: 4.7 us -> none  [the longest x31 2.37 us: combine(): factor_second = jnp.exp(second[index] - row_max)]
    all_gather x1 -> x0, waiting for transfers between devices: 3.97 us -> none  [collected_together(): both, at, found = (lax.all_gather(jnp.concatenate(lines), axis), 0, {})]
    another operation x1 -> x0, local copies, waits for them, and re-layouts: 3.13 us -> none  [collected_together(): found[k] = piece[:, :leaves[k].size].reshape(-1, *leaves[k].shape)]
  transfers between devices with their start and end apart: 1 -> 0, of which waited for: 1 -> 0; matrix products, arithmetic and copies ran while one was open for 2% -> 0% of each run, Pallas kernels for 0% -> 0%
where the time goes in v1:
time: 83.8 us; the launch traced here: 83.6 us
  Pallas kernels  82.1 us (98%)
  local copies, waits for them, and re-layouts  1.47 us (2%)
    pallas_call x1, Pallas kernels, on_device(): pl.pallas_call(functools.partial(kernel, n), name='decode', out_shape=jax...  82.1 us

profile of v1, /device:TPU:40, one launch (start us, length us, event | category | flops | bytes accessed | tf_op | source)
XLA Modules:
  0.0 83.6 jit_solution(5098025700541358885)
XLA Ops:
  0.0 82.1 %decode.1 = bf16[16,16,128]{2,1,0:T(8,128)(2,1)} custom-call(bf16[16,16,128]{2,1,0:T(8,128)(2,1)} %q_ref.1, bf16[16,2,256,128]{3,2,1,0:T(8,128)(2,1)} %k_hbm.1, bf16[16,2,256,128]{3,2,1,0:T(8,128)(2,1)} %v_hbm.1, f32[2,16,16]{2,1,0:T(8,128)} %gate_ref.1, s32[16]{0:T(128)} %length_ref.1, s32[16,2,16]{2,1,0:T(2,128)} %chosen_ref.1, s32[2,16]{1,0:T(2,128)} %bitcast.1), custom_call_target="tpu_custom_call" | custom-call | tf_op jit(solution)/shard_map/decode/pallas_call | solution.py:293
  82.1 1.5 %copy.9 = bf16[16,16,128]{2,1,0:T(8,128)(2,1)} copy(bf16[16,16,128]{2,1,0:T(8,128)(2,1)} %decode.1) | data formatting | bytes 131072

commit v2 on v1

--- a/solution.py
+++ b/solution.py
@@ -12,6 +12,7 @@
 STRIDE = 4
 NEAR = (-1, 1, 2)
 CHUNK = 4
+LOADS = 2
 PIECE = 32
 NEG = -1e30
 MESH = pl.DeviceIdType.MESH
@@ -62,12 +63,14 @@
     board,
     gate_pad,
     gates,
+    scores,
     k_sem,
     v_sem,
     a_send,
     a_recv,
     b_send,
-    b_recv,
+    hop_recv,
+    near_recv,
 ):
     me = lax.axis_index("seq")
     sign = 1 - 2 * lax.axis_index("batch")
@@ -98,16 +101,14 @@
         for offset in (-distance, distance):
             pl.semaphore_signal(barrier, inc=1, device_id={"seq": at(offset)}, device_id_type=MESH)
 
-    def loads(c):
-        part = pl.ds(c * CHUNK, CHUNK)
-        return (
-            pltpu.make_async_copy(k_hbm.at[part], k_buf.at[part], k_sem.at[c]),
-            pltpu.make_async_copy(v_hbm.at[part], v_buf.at[part], v_sem.at[c]),
-        )
-
-    for c in range(rows // CHUNK):
-        for copy in loads(c):
-            copy.start()
+    def load(which, c):
+        part = pl.ds(c * (rows // LOADS), rows // LOADS)
+        source, target, sem = (v_hbm, v_buf, v_sem) if which else (k_hbm, k_buf, k_sem)
+        return pltpu.make_async_copy(source.at[part], target.at[part], sem.at[c])
+
+    for which in range(2):
+        for c in range(LOADS):
+            load(which, c).start()
 
     gate_pad[...] = jnp.zeros_like(gate_pad)
     for branch in range(2):
@@ -129,10 +130,7 @@
     first = me * local
 
     def one_pair(b, h, live, root):
-        scores = lax.dot_general(
-            q_ref[b], k_buf[b, h], (((1,), (1,)), ((), ())), preferred_element_type=jnp.float32
-        )[h * group : (h + 1) * group] * scale
-        parts = [scores[:, j * BLOCK : (j + 1) * BLOCK] for j in range(local)]
+        parts = [scores[b, h, :, j * BLOCK : (j + 1) * BLOCK] for j in range(local)]
         chosen = chosen_ref[b, h : h + 1, :]
         listed = slot < count_ref[h, b]
         masks = []
@@ -187,47 +185,51 @@
                 logs = jnp.where(lane == branch * heads + h, pairs[h][branch][1], logs)
         sent[b, 2 * tile :] = split_logs(logs)
 
-    def one_chunk(c, carry):
-        for copy in loads(c):
-            copy.wait()
+    def score_chunk(c, carry):
+        for i in range(CHUNK):
+            b = c * CHUNK + i
+            for h in range(heads):
+                product = lax.dot_general(
+                    q_ref[b], k_buf[b, h], (((1,), (1,)), ((), ())), preferred_element_type=jnp.float32
+                )
+                scores[b, h] = product[h * group : (h + 1) * group] * scale
+        return carry
+
+    def value_chunk(c, carry):
         for i in range(CHUNK):
             one_row(c * CHUNK + i)
         return carry
 
-    lax.fori_loop(0, rows // CHUNK, one_chunk, 0)
+    per_load = rows // LOADS // CHUNK
+    for which, chunk in ((0, score_chunk), (1, value_chunk)):
+        for c in range(LOADS):
+            load(which, c).wait()
+            lax.fori_loop(c * per_load, (c + 1) * per_load, chunk, 0)
 
     pl.semaphore_wait(barrier, 2 * half)
-    offsets = [d for d in range(-half, half) if d != 0]
-    first_copies = []
-    for i, offset in enumerate(sorted(offsets, key=lambda d: -abs(d))):
+    offsets = sorted((d for d in range(-half, half) if d != 0), key=lambda d: -abs(d))
+    for i, offset in enumerate(offsets):
         target = at(offset)
-        copy = remote(
-            sent.at[lax.rem(target, window)],
-            landed.at[offset + half],
-            a_send.at[i],
-            a_recv.at[offset + half],
-            target,
-        )
-        copy.start()
-        first_copies.append(copy)
-    for copy in first_copies:
-        copy.wait_recv()
+        remote(sent.at[lax.rem(target, window)], landed.at[i], a_send, a_recv, target).start()
+    arrivals = pl.ds(0, len(offsets))
+    first_copies = remote(sent.at[arrivals], landed.at[arrivals], a_send, a_recv, at(1))
+    first_copies.wait_recv()
 
     mine = lax.rem(me, window)
     logs = [
-        join_logs(sent[mine, 2 * tile :] if d == 0 else landed[d + half, 2 * tile :])
-        for d in range(-half, half)
+        join_logs(sent[mine, 2 * tile :] if i < 0 else landed[i, 2 * tile :])
+        for i in range(-1, len(offsets))
     ]
     top = functools.reduce(jnp.maximum, logs)
     shares = [jnp.exp(x - top) for x in logs]
     total = functools.reduce(jnp.add, shares)
     merged = [jnp.zeros((group, width), jnp.float32) for _ in range(2 * heads)]
     inverse = 1.0 / total
-    for share, d in zip(shares, range(-half, half)):
+    for share, i in zip(shares, range(-1, len(offsets))):
         share = share * inverse
         for c in range(0, 2 * heads, heads):
             part = pl.ds(c * group, tile)
-            values = (sent[mine, part] if d == 0 else landed[d + half, part]).astype(jnp.float32)
+            values = (sent[mine, part] if i < 0 else landed[i, part]).astype(jnp.float32)
             for h in range(heads):
                 merged[c + h] += column(share, c + h) * values[h * group : (h + 1) * group]
     for branch in range(2):
@@ -236,32 +238,27 @@
         ).astype(jnp.bfloat16)
     board[me, 2 * tile :] = split_logs(jnp.where(lane < 2 * heads, top + jnp.log(total), 0.0))
 
-    def broadcast(owner, offset, number):
-        return remote(board.at[owner], board.at[owner], b_send.at[number], b_recv.at[owner], at(offset))
-
     steps = []
     for distance in range(STRIDE, n // 2, STRIDE):
         steps += [distance, -distance]
     steps.append(n // 2)
-    second_copies = []
-
-    def start(owner, offset):
-        copy = broadcast(owner, offset, len(second_copies))
-        copy.start()
-        second_copies.append(copy)
-
-    for offset in reversed(steps):
-        start(me, offset)
-    for near in NEAR:
-        start(me, near)
-    for offset in steps:
+
+    def hop(number, owner):
+        return remote(board.at[owner], board.at[owner], b_send, hop_recv.at[number], at(steps[number]))
+
+    def pass_on(owner):
+        for near in NEAR:
+            remote(board.at[owner], board.at[owner], b_send, near_recv, at(near)).start()
+
+    for number in reversed(range(len(steps))):
+        hop(number, me).start()
+    pass_on(me)
+    for number, offset in enumerate(steps):
         owner = at(-offset)
-        broadcast(owner, offset, 0).wait_recv()
-        for near in NEAR:
-            start(owner, near)
-    for offset in [0] + steps:
-        for near in NEAR:
-            broadcast(at(-offset - near), near, 0).wait_recv()
+        hop(number, owner).wait_recv()
+        pass_on(owner)
+    passed = pl.ds(0, len(NEAR) * (len(steps) + 1))
+    remote(board.at[passed], board.at[passed], b_send, near_recv, at(1)).wait_recv()
 
     for b in range(rows):
         logs = [join_logs(board[s * window + b, 2 * tile :]) for s in range(sources)]
@@ -277,8 +274,9 @@
                     mixed[h] += column(share, branch * heads + h) * values[h * group : (h + 1) * group]
         out_ref[b] = jnp.concatenate(mixed, axis=0).astype(jnp.bfloat16)
 
-    for copy in first_copies + second_copies:
-        copy.wait_send()
+    first_copies.wait_send()
+    everything = pl.ds(0, n - 1)
+    remote(board.at[everything], board.at[everything], b_send, near_recv, at(1)).wait_send()
 
 
 def on_device(n, queries, key_cache, value_cache, gate_logits, lengths, chosen, counts):
@@ -304,12 +302,14 @@
             pltpu.VMEM((n, lines, width), jnp.bfloat16),
             pltpu.VMEM((width, width), jnp.float32),
             pltpu.VMEM((rows, group, width), jnp.float32),
-            pltpu.SemaphoreType.DMA((rows // CHUNK,)),
-            pltpu.SemaphoreType.DMA((rows // CHUNK,)),
-            pltpu.SemaphoreType.DMA((window,)),
-            pltpu.SemaphoreType.DMA((window,)),
-            pltpu.SemaphoreType.DMA((relays + len(NEAR) * (relays + 1),)),
-            pltpu.SemaphoreType.DMA((n,)),
+            pltpu.VMEM((rows, heads, group, context), jnp.float32),
+            pltpu.SemaphoreType.DMA((LOADS,)),
+            pltpu.SemaphoreType.DMA((LOADS,)),
+            pltpu.SemaphoreType.DMA,
+            pltpu.SemaphoreType.DMA,
+            pltpu.SemaphoreType.DMA,
+            pltpu.SemaphoreType.DMA((relays,)),
+            pltpu.SemaphoreType.DMA,
         ],
         compiler_params=pltpu.CompilerParams(collective_id=0, has_side_effects=True),
     )(queries, key_cache, value_cache, gate_logits, lengths, chosen, counts.T)

time: 83.8 us -> 77.2 us (0.921)
  Pallas kernels: 82.1 us -> 75.5 us
    pallas_call x1, Pallas kernels: 82.1 us -> 75.5 us  [on_device(): pl.pallas_call(functools.partial(kernel, n), name='decode', out_shape=jax...]
where the time goes in v2:
time: 77.2 us; the launch traced here: 77 us
  Pallas kernels  75.5 us (98%)
  local copies, waits for them, and re-layouts  1.47 us (2%)
    pallas_call x1, Pallas kernels, on_device(): pl.pallas_call(functools.partial(kernel, n), name='decode', out_shape=jax...  75.5 us

profile of v2, /device:TPU:40, one launch (start us, length us, event | category | flops | bytes accessed | tf_op | source)
XLA Modules:
  0.0 77.0 jit_solution(308412722157033971)
XLA Ops:
  0.0 75.5 %decode.1 = bf16[16,16,128]{2,1,0:T(8,128)(2,1)} custom-call(bf16[16,16,128]{2,1,0:T(8,128)(2,1)} %q_ref.1, bf16[16,2,256,128]{3,2,1,0:T(8,128)(2,1)} %k_hbm.1, bf16[16,2,256,128]{3,2,1,0:T(8,128)(2,1)} %v_hbm.1, f32[2,16,16]{2,1,0:T(8,128)} %gate_ref.1, s32[16]{0:T(128)} %length_ref.1, s32[16,2,16]{2,1,0:T(2,128)} %chosen_ref.1, s32[2,16]{1,0:T(2,128)} %bitcast.1), custom_call_target="tpu_custom_call" | custom-call | tf_op jit(solution)/shard_map/decode/pallas_call | solution.py:291
  75.5 1.5 %copy.9 = bf16[16,16,128]{2,1,0:T(8,128)(2,1)} copy(bf16[16,16,128]{2,1,0:T(8,128)(2,1)} %decode.1) | data formatting | bytes 131072

commit v3 on v2

--- a/solution.py
+++ b/solution.py
@@ -9,8 +9,9 @@
 from jax.sharding import PartitionSpec as P
 
 BLOCK = 128
+WINDOW = 8
+ROOT = 1
 STRIDE = 4
-NEAR = (-1, 1, 2)
 CHUNK = 4
 LOADS = 2
 PIECE = 32
@@ -69,22 +70,23 @@
     a_send,
     a_recv,
     b_send,
-    hop_recv,
-    near_recv,
+    b_recv,
+    c_send,
+    c_recv,
 ):
     me = lax.axis_index("seq")
     sign = 1 - 2 * lax.axis_index("batch")
     rows, heads, context, width = k_buf.shape
     group = q_ref.shape[1] // heads
     local = context // BLOCK
-    window = rows
-    half = window // 2
-    sources = n // window
+    half = WINDOW // 2
+    sources = n // WINDOW
+    per = rows // WINDOW
     tile = heads * group
     scale = 1.0 / math.sqrt(width)
 
     def at(offset):
-        return lax.rem(me + sign * offset + 2 * n, n)
+        return lax.rem(me + sign * offset + n, n)
 
     def remote(src, dst, send, recv, target):
         return pltpu.make_async_remote_copy(
@@ -96,9 +98,17 @@
             device_id_type=MESH,
         )
 
+    root = ROOT
+    away = lax.rem(sign * (root - me) + n, n)
+    outside = (away > half) & (away < n - half)
     barrier = pltpu.get_barrier_semaphore()
     for distance in range(half, 0, -1):
         for offset in (-distance, distance):
+            pl.semaphore_signal(barrier, inc=1, device_id={"seq": at(offset)}, device_id_type=MESH)
+
+    @pl.when(me == root)
+    def _():
+        for offset in range(half + 1, n - half):
             pl.semaphore_signal(barrier, inc=1, device_id={"seq": at(offset)}, device_id_type=MESH)
 
     def load(which, c):
@@ -116,15 +126,16 @@
         gate_pad[branch * rows : (branch + 1) * rows, : heads * group] = 1.0 / (1.0 + jnp.exp(-logits))
     turned = gate_pad[...].T
     lane = iota((group, width), 1)
-    for b in range(rows):
+    for block in range(WINDOW):
         packed = jnp.zeros((group, width), jnp.float32)
-        for branch in range(2):
-            for h in range(heads):
-                c = branch * heads + h
-                here = turned[h * group : (h + 1) * group]
-                moved = pltpu.roll(here, (c - (1 - branch) * rows - b) % width, 1)
-                packed = jnp.where(lane == c, moved, packed)
-        gates[b] = packed
+        for k in range(per):
+            for branch in range(2):
+                for h in range(heads):
+                    c = (2 * k + branch) * heads + h
+                    here = turned[h * group : (h + 1) * group]
+                    moved = pltpu.roll(here, (c - (1 - branch) * rows - block * per - k) % width, 1)
+                    packed = jnp.where(lane == c, moved, packed)
+        gates[block] = packed
 
     slot = iota((1, chosen_ref.shape[2]), 1)
     first = me * local
@@ -168,7 +179,7 @@
             result.append((value / safe, jnp.where(some, top_of + jnp.log(safe), NEG)))
         return result
 
-    def one_row(b):
+    def one_row(b, block, k, logs):
         length = length_ref[b]
         live, root = [], []
         for j in range(local):
@@ -177,13 +188,12 @@
             filled = jnp.clip(length - start, 1, BLOCK).astype(jnp.float32)
             root.append(1.0 / jnp.sqrt(jnp.full((group, 1), filled, jnp.float32)))
         pairs = [one_pair(b, h, live, root) for h in range(heads)]
-        logs = jnp.zeros((group, width), jnp.float32)
         for branch in range(2):
             values = jnp.concatenate([pairs[h][branch][0] for h in range(heads)], axis=0)
-            sent[b, branch * tile : (branch + 1) * tile] = values.astype(jnp.bfloat16)
+            sent[block, pl.ds((2 * k + branch) * tile, tile)] = values.astype(jnp.bfloat16)
             for h in range(heads):
-                logs = jnp.where(lane == branch * heads + h, pairs[h][branch][1], logs)
-        sent[b, 2 * tile :] = split_logs(logs)
+                logs = jnp.where(lane == (2 * k + branch) * heads + h, pairs[h][branch][1], logs)
+        return logs
 
     def score_chunk(c, carry):
         for i in range(CHUNK):
@@ -196,8 +206,12 @@
         return carry
 
     def value_chunk(c, carry):
-        for i in range(CHUNK):
-            one_row(c * CHUNK + i)
+        for i in range(CHUNK // per):
+            block = c * (CHUNK // per) + i
+            logs = jnp.zeros((group, width), jnp.float32)
+            for k in range(per):
+                logs = one_row(block * per + k, block, k, logs)
+            sent[block, 2 * per * tile :] = split_logs(logs)
         return carry
 
     per_load = rows // LOADS // CHUNK
@@ -206,109 +220,116 @@
             load(which, c).wait()
             lax.fori_loop(c * per_load, (c + 1) * per_load, chunk, 0)
 
-    pl.semaphore_wait(barrier, 2 * half)
+    pl.semaphore_wait(barrier, 2 * half + outside.astype(jnp.int32))
     offsets = sorted((d for d in range(-half, half) if d != 0), key=lambda d: -abs(d))
     for i, offset in enumerate(offsets):
         target = at(offset)
-        remote(sent.at[lax.rem(target, window)], landed.at[i], a_send, a_recv, target).start()
+        remote(sent.at[lax.rem(target, WINDOW)], landed.at[i], a_send, a_recv, target).start()
     arrivals = pl.ds(0, len(offsets))
     first_copies = remote(sent.at[arrivals], landed.at[arrivals], a_send, a_recv, at(1))
     first_copies.wait_recv()
 
-    mine = lax.rem(me, window)
-    logs = [
-        join_logs(sent[mine, 2 * tile :] if i < 0 else landed[i, 2 * tile :])
-        for i in range(-1, len(offsets))
-    ]
+    mine = lax.rem(me, WINDOW)
+    logs = [join_logs(sent[mine, 2 * per * tile :] if i < 0 else landed[i, 2 * per * tile :]) for i in range(-1, len(offsets))]
     top = functools.reduce(jnp.maximum, logs)
     shares = [jnp.exp(x - top) for x in logs]
     total = functools.reduce(jnp.add, shares)
-    merged = [jnp.zeros((group, width), jnp.float32) for _ in range(2 * heads)]
     inverse = 1.0 / total
+    merged = [jnp.zeros((group, width), jnp.float32) for _ in range(2 * per * heads)]
     for share, i in zip(shares, range(-1, len(offsets))):
         share = share * inverse
-        for c in range(0, 2 * heads, heads):
+        for c in range(0, len(merged), heads):
             part = pl.ds(c * group, tile)
             values = (sent[mine, part] if i < 0 else landed[i, part]).astype(jnp.float32)
             for h in range(heads):
                 merged[c + h] += column(share, c + h) * values[h * group : (h + 1) * group]
-    for branch in range(2):
-        board[me, branch * tile : (branch + 1) * tile] = jnp.concatenate(
-            merged[branch * heads : (branch + 1) * heads], axis=0
-        ).astype(jnp.bfloat16)
-    board[me, 2 * tile :] = split_logs(jnp.where(lane < 2 * heads, top + jnp.log(total), 0.0))
-
-    steps = []
-    for distance in range(STRIDE, n // 2, STRIDE):
-        steps += [distance, -distance]
-    steps.append(n // 2)
-
-    def hop(number, owner):
-        return remote(board.at[owner], board.at[owner], b_send, hop_recv.at[number], at(steps[number]))
-
-    def pass_on(owner):
-        for near in NEAR:
-            remote(board.at[owner], board.at[owner], b_send, near_recv, at(near)).start()
-
-    for number in reversed(range(len(steps))):
-        hop(number, me).start()
-    pass_on(me)
-    for number, offset in enumerate(steps):
-        owner = at(-offset)
-        hop(number, owner).wait_recv()
-        pass_on(owner)
-    passed = pl.ds(0, len(NEAR) * (len(steps) + 1))
-    remote(board.at[passed], board.at[passed], b_send, near_recv, at(1)).wait_recv()
-
-    for b in range(rows):
-        logs = [join_logs(board[s * window + b, 2 * tile :]) for s in range(sources)]
-        top = functools.reduce(jnp.maximum, logs)
-        shares = [jnp.exp(x - top) for x in logs]
-        factor = gates[b] / functools.reduce(jnp.add, shares)
-        mixed = [jnp.zeros((group, width), jnp.float32) for _ in range(heads)]
-        for s, share in enumerate(shares):
-            share = share * factor
-            for branch in range(2):
-                values = board[s * window + b, branch * tile : (branch + 1) * tile].astype(jnp.float32)
-                for h in range(heads):
-                    mixed[h] += column(share, branch * heads + h) * values[h * group : (h + 1) * group]
-        out_ref[b] = jnp.concatenate(mixed, axis=0).astype(jnp.bfloat16)
+    for c in range(0, len(merged), heads):
+        board[me, c * group : c * group + tile] = jnp.concatenate(merged[c : c + heads], axis=0).astype(jnp.bfloat16)
+    board[me, 2 * per * tile :] = split_logs(jnp.where(lane < len(merged), top + jnp.log(total), 0.0))
+
+    relays = n // STRIDE
+    up = relays // 2 + 1
+    split = relays // 4
+
+    def spread(k):
+        steps = [STRIDE] if k < up else []
+        steps += [-(split + 1) * STRIDE] if k == split else []
+        steps += [-STRIDE] if up + 1 < k else []
+        copies = []
+        for i, step in enumerate([-1] + steps + [1, 2]):
+            target = (ROOT + k * STRIDE + step) % n
+            copies.append(remote(out_ref, out_ref, c_send.at[i], c_recv, target))
+            copies[-1].start()
+        for copy in copies:
+            copy.wait_send()
+
+    @pl.when(me != root)
+    def _():
+        block = remote(board.at[me], board.at[me], b_send, b_recv, root)
+        block.start()
+        block.wait_send()
+        remote(out_ref, out_ref, c_send.at[0], c_recv, root).wait_recv()
+        for k in range(1, relays):
+
+            @pl.when(me == (ROOT + k * STRIDE) % n)
+            def _(k=k):
+                spread(k)
+
+    @pl.when(me == root)
+    def _():
+        others = pl.ds(0, n - 1)
+        remote(board.at[others], board.at[others], b_send, b_recv, at(1)).wait_recv()
+        for block in range(WINDOW):
+            logs = [join_logs(board[s * WINDOW + block, 2 * per * tile :]) for s in range(sources)]
+            top = functools.reduce(jnp.maximum, logs)
+            shares = [jnp.exp(x - top) for x in logs]
+            inverse = 1.0 / functools.reduce(jnp.add, shares)
+            factor = gates[block] * inverse
+            shares = [x * factor for x in shares]
+            for k in range(per):
+                mixed = [jnp.zeros((group, width), jnp.float32) for _ in range(heads)]
+                for s, share in enumerate(shares):
+                    for branch in range(2):
+                        c = (2 * k + branch) * heads
+                        values = board[s * WINDOW + block, c * group : c * group + tile].astype(jnp.float32)
+                        for h in range(heads):
+                            mixed[h] += column(share, c + h) * values[h * group : (h + 1) * group]
+                out_ref[block * per + k] = jnp.concatenate(mixed, axis=0).astype(jnp.bfloat16)
+
+        spread(0)
 
     first_copies.wait_send()
-    everything = pl.ds(0, n - 1)
-    remote(board.at[everything], board.at[everything], b_send, near_recv, at(1)).wait_send()
 
 
 def on_device(n, queries, key_cache, value_cache, gate_logits, lengths, chosen, counts):
     rows, heads, context, width = key_cache.shape
     group = queries.shape[1] // heads
-    window = rows
-    lines = 2 * heads * group + group
-    relays = len(range(STRIDE, n // 2, STRIDE)) * 2 + 1
+    lines = rows // WINDOW * 2 * heads * group + group
     vmem = pl.BlockSpec(memory_space=pltpu.VMEM)
     smem = pl.BlockSpec(memory_space=pltpu.SMEM)
     anywhere = pl.BlockSpec(memory_space=pl.ANY)
     return pl.pallas_call(
         functools.partial(kernel, n),
         name="decode",
-        out_shape=jax.ShapeDtypeStruct(queries.shape, jnp.bfloat16),
+        out_shape=pltpu.VMEM(queries.shape, jnp.bfloat16),
         in_specs=[vmem, anywhere, anywhere, vmem, smem, vmem, smem],
         out_specs=vmem,
         scratch_shapes=[
             pltpu.VMEM(key_cache.shape, jnp.bfloat16),
             pltpu.VMEM(value_cache.shape, jnp.bfloat16),
-            pltpu.VMEM((rows, lines, width), jnp.bfloat16),
-            pltpu.VMEM((window, lines, width), jnp.bfloat16),
+            pltpu.VMEM((WINDOW, lines, width), jnp.bfloat16),
+            pltpu.VMEM((WINDOW - 1, lines, width), jnp.bfloat16),
             pltpu.VMEM((n, lines, width), jnp.bfloat16),
             pltpu.VMEM((width, width), jnp.float32),
-            pltpu.VMEM((rows, group, width), jnp.float32),
+            pltpu.VMEM((WINDOW, group, width), jnp.float32),
             pltpu.VMEM((rows, heads, group, context), jnp.float32),
             pltpu.SemaphoreType.DMA((LOADS,)),
             pltpu.SemaphoreType.DMA((LOADS,)),
             pltpu.SemaphoreType.DMA,
             pltpu.SemaphoreType.DMA,
             pltpu.SemaphoreType.DMA,
-            pltpu.SemaphoreType.DMA((relays,)),
+            pltpu.SemaphoreType.DMA,
+            pltpu.SemaphoreType.DMA((5,)),
             pltpu.SemaphoreType.DMA,
         ],
         compiler_params=pltpu.CompilerParams(collective_id=0, has_side_effects=True),

time: 77.2 us -> 66.2 us (0.86)
  Pallas kernels: 75.5 us -> 65.4 us
  local copies, waits for them, and re-layouts: 1.47 us -> 0.63 us
    pallas_call x1, Pallas kernels: 75.5 us -> 65.4 us  [on_device(): pl.pallas_call(functools.partial(kernel, n), name='decode', out_shape=plt...]
    unnamed x1, local copies, waits for them, and re-layouts: 1.47 us -> 0.63 us
where the time goes in v3:
time: 66.2 us; the launch traced here: 66 us
  Pallas kernels  65.4 us (99%)
    pallas_call x1, Pallas kernels, on_device(): pl.pallas_call(functools.partial(kernel, n), name='decode', out_shape=plt...  65.4 us

profile of v3, /device:TPU:40, one launch (start us, length us, event | category | flops | bytes accessed | tf_op | source)
XLA Modules:
  0.0 66.0 jit_solution(14393631261413087163)
XLA Ops:
  0.0 65.4 %decode.1 = bf16[16,16,128]{2,1,0:T(8,128)(2,1)S(1)} custom-call(bf16[16,16,128]{2,1,0:T(8,128)(2,1)} %q_ref.1, bf16[16,2,256,128]{3,2,1,0:T(8,128)(2,1)} %k_hbm.1, bf16[16,2,256,128]{3,2,1,0:T(8,128)(2,1)} %v_hbm.1, f32[2,16,16]{2,1,0:T(8,128)} %gate_ref.1, s32[16]{0:T(128)} %length_ref.1, s32[16,2,16]{2,1,0:T(2,128)} %chosen_ref.1, s32[2,16]{1,0:T(2,128)} %bitcast.1), custom_call_target="tpu_custom_call" | custom-call | tf_op jit(solution)/shard_map/decode/pallas_call | solution.py:311
  65.4 0.6 copy.9

commit v4 on v3

--- a/solution.py
+++ b/solution.py
@@ -12,6 +12,7 @@
 WINDOW = 8
 ROOT = 1
 STRIDE = 4
+PARTS = 4
 CHUNK = 4
 LOADS = 2
 PIECE = 32
@@ -49,14 +50,19 @@
 
 def kernel(
     n,
-    q_ref,
+    q_hbm,
     k_hbm,
     v_hbm,
+    gate_hbm,
+    length_hbm,
+    chosen_hbm,
+    count_hbm,
+    out_ref,
+    q_ref,
     gate_ref,
     length_ref,
     chosen_ref,
     count_ref,
-    out_ref,
     k_buf,
     v_buf,
     sent,
@@ -65,6 +71,7 @@
     gate_pad,
     gates,
     scores,
+    in_sem,
     k_sem,
     v_sem,
     a_send,
@@ -75,7 +82,6 @@
     c_recv,
 ):
     me = lax.axis_index("seq")
-    sign = 1 - 2 * lax.axis_index("batch")
     rows, heads, context, width = k_buf.shape
     group = q_ref.shape[1] // heads
     local = context // BLOCK
@@ -86,7 +92,7 @@
     scale = 1.0 / math.sqrt(width)
 
     def at(offset):
-        return lax.rem(me + sign * offset + n, n)
+        return lax.rem(me + offset + n, n)
 
     def remote(src, dst, send, recv, target):
         return pltpu.make_async_remote_copy(
@@ -98,8 +104,33 @@
             device_id_type=MESH,
         )
 
+    def load(which, c):
+        part = pl.ds(c * (rows // LOADS), rows // LOADS)
+        source, target, sem = (v_hbm, v_buf, v_sem) if which else (k_hbm, k_buf, k_sem)
+        return pltpu.make_async_copy(source.at[part], target.at[part], sem.at[c])
+
+    small = [
+        pltpu.make_async_copy(source, target, in_sem.at[i])
+        for i, (source, target) in enumerate(
+            (
+                (q_hbm, q_ref),
+                (length_hbm, length_ref),
+                (chosen_hbm, chosen_ref),
+                (count_hbm, count_ref),
+                (gate_hbm, gate_ref),
+            )
+        )
+    ]
+    small[0].start()
+    for c in range(LOADS):
+        load(0, c).start()
+    for copy in small[1:]:
+        copy.start()
+    for c in range(LOADS):
+        load(1, c).start()
+
     root = ROOT
-    away = lax.rem(sign * (root - me) + n, n)
+    away = lax.rem(root - me + n, n)
     outside = (away > half) & (away < n - half)
     barrier = pltpu.get_barrier_semaphore()
     for distance in range(half, 0, -1):
@@ -111,32 +142,7 @@
         for offset in range(half + 1, n - half):
             pl.semaphore_signal(barrier, inc=1, device_id={"seq": at(offset)}, device_id_type=MESH)
 
-    def load(which, c):
-        part = pl.ds(c * (rows // LOADS), rows // LOADS)
-        source, target, sem = (v_hbm, v_buf, v_sem) if which else (k_hbm, k_buf, k_sem)
-        return pltpu.make_async_copy(source.at[part], target.at[part], sem.at[c])
-
-    for which in range(2):
-        for c in range(LOADS):
-            load(which, c).start()
-
-    gate_pad[...] = jnp.zeros_like(gate_pad)
-    for branch in range(2):
-        logits = gate_ref[branch]
-        gate_pad[branch * rows : (branch + 1) * rows, : heads * group] = 1.0 / (1.0 + jnp.exp(-logits))
-    turned = gate_pad[...].T
     lane = iota((group, width), 1)
-    for block in range(WINDOW):
-        packed = jnp.zeros((group, width), jnp.float32)
-        for k in range(per):
-            for branch in range(2):
-                for h in range(heads):
-                    c = (2 * k + branch) * heads + h
-                    here = turned[h * group : (h + 1) * group]
-                    moved = pltpu.roll(here, (c - (1 - branch) * rows - block * per - k) % width, 1)
-                    packed = jnp.where(lane == c, moved, packed)
-        gates[block] = packed
-
     slot = iota((1, chosen_ref.shape[2]), 1)
     first = me * local
 
@@ -215,13 +221,17 @@
         return carry
 
     per_load = rows // LOADS // CHUNK
+    small[0].wait()
     for which, chunk in ((0, score_chunk), (1, value_chunk)):
+        if which:
+            for copy in small[1:]:
+                copy.wait()
         for c in range(LOADS):
             load(which, c).wait()
             lax.fori_loop(c * per_load, (c + 1) * per_load, chunk, 0)
 
     pl.semaphore_wait(barrier, 2 * half + outside.astype(jnp.int32))
-    offsets = sorted((d for d in range(-half, half) if d != 0), key=lambda d: -abs(d))
+    offsets = sorted((d for d in range(1 - half, half + 1) if d != 0), key=lambda d: -abs(d))
     for i, offset in enumerate(offsets):
         target = at(offset)
         remote(sent.at[lax.rem(target, WINDOW)], landed.at[i], a_send, a_recv, target).start()
@@ -256,7 +266,7 @@
         steps += [-(split + 1) * STRIDE] if k == split else []
         steps += [-STRIDE] if up + 1 < k else []
         copies = []
-        for i, step in enumerate([-1] + steps + [1, 2]):
+        for i, step in enumerate(([-1] if k else []) + steps + [1, 2]):
             target = (ROOT + k * STRIDE + step) % n
             copies.append(remote(out_ref, out_ref, c_send.at[i], c_recv, target))
             copies[-1].start()
@@ -277,8 +287,25 @@
 
     @pl.when(me == root)
     def _():
+        gate_pad[...] = jnp.zeros_like(gate_pad)
+        for branch in range(2):
+            logits = gate_ref[branch]
+            gate_pad[branch * rows : (branch + 1) * rows, : heads * group] = 1.0 / (1.0 + jnp.exp(-logits))
+        turned = gate_pad[...].T
+        for block in range(WINDOW):
+            packed = jnp.zeros((group, width), jnp.float32)
+            for k in range(per):
+                for branch in range(2):
+                    for h in range(heads):
+                        c = (2 * k + branch) * heads + h
+                        here = turned[h * group : (h + 1) * group]
+                        moved = pltpu.roll(here, (c - (1 - branch) * rows - block * per - k) % width, 1)
+                        packed = jnp.where(lane == c, moved, packed)
+            gates[block] = packed
+
         others = pl.ds(0, n - 1)
         remote(board.at[others], board.at[others], b_send, b_recv, at(1)).wait_recv()
+        early = []
         for block in range(WINDOW):
             logs = [join_logs(board[s * WINDOW + block, 2 * per * tile :]) for s in range(sources)]
             top = functools.reduce(jnp.maximum, logs)
@@ -295,8 +322,15 @@
                         for h in range(heads):
                             mixed[h] += column(share, c + h) * values[h * group : (h + 1) * group]
                 out_ref[block * per + k] = jnp.concatenate(mixed, axis=0).astype(jnp.bfloat16)
+            if (block + 1) % (WINDOW // PARTS) == 0:
+                part = pl.ds((block + 1 - WINDOW // PARTS) * per, rows // PARTS)
+                send = c_send.at[5 + block // (WINDOW // PARTS)]
+                early.append(remote(out_ref.at[part], out_ref.at[part], send, c_recv, (ROOT - 1) % n))
+                early[-1].start()
 
         spread(0)
+        for copy in early:
+            copy.wait_send()
 
     first_copies.wait_send()
 
@@ -306,15 +340,19 @@
     group = queries.shape[1] // heads
     lines = rows // WINDOW * 2 * heads * group + group
     vmem = pl.BlockSpec(memory_space=pltpu.VMEM)
-    smem = pl.BlockSpec(memory_space=pltpu.SMEM)
     anywhere = pl.BlockSpec(memory_space=pl.ANY)
     return pl.pallas_call(
         functools.partial(kernel, n),
         name="decode",
         out_shape=pltpu.VMEM(queries.shape, jnp.bfloat16),
-        in_specs=[vmem, anywhere, anywhere, vmem, smem, vmem, smem],
+        in_specs=[anywhere] * 7,
         out_specs=vmem,
         scratch_shapes=[
+            pltpu.VMEM(queries.shape, jnp.bfloat16),
+            pltpu.VMEM(gate_logits.shape, jnp.float32),
+            pltpu.SMEM(lengths.shape, jnp.int32),
+            pltpu.VMEM(chosen.shape, jnp.int32),
+            pltpu.SMEM((heads, rows), jnp.int32),
             pltpu.VMEM(key_cache.shape, jnp.bfloat16),
             pltpu.VMEM(value_cache.shape, jnp.bfloat16),
             pltpu.VMEM((WINDOW, lines, width), jnp.bfloat16),
@@ -323,13 +361,14 @@
             pltpu.VMEM((width, width), jnp.float32),
             pltpu.VMEM((WINDOW, group, width), jnp.float32),
             pltpu.VMEM((rows, heads, group, context), jnp.float32),
+            pltpu.SemaphoreType.DMA((5,)),
             pltpu.SemaphoreType.DMA((LOADS,)),
             pltpu.SemaphoreType.DMA((LOADS,)),
             pltpu.SemaphoreType.DMA,
             pltpu.SemaphoreType.DMA,
             pltpu.SemaphoreType.DMA,
             pltpu.SemaphoreType.DMA,
-            pltpu.SemaphoreType.DMA((5,)),
+            pltpu.SemaphoreType.DMA((5 + PARTS,)),
             pltpu.SemaphoreType.DMA,
         ],
         compiler_params=pltpu.CompilerParams(collective_id=0, has_side_effects=True),

time: 66.2 us -> 64.6 us (0.976)
  Pallas kernels: 65.4 us -> 63.8 us
    pallas_call x1, Pallas kernels: 65.4 us -> 63.8 us  [on_device(): pl.pallas_call(functools.partial(kernel, n), name='decode', out_shape=plt...]
where the time goes in v4:
time: 64.6 us; the launch traced here: 64.4 us
  Pallas kernels  63.8 us (99%)
    pallas_call x1, Pallas kernels, on_device(): pl.pallas_call(functools.partial(kernel, n), name='decode', out_shape=plt...  63.8 us

profile of v4, /device:TPU:40, one launch (start us, length us, event | category | flops | bytes accessed | tf_op | source)
XLA Modules:
  0.0 64.4 jit_solution(5633783881319900380)
XLA Ops:
  0.0 63.8 %decode.1 = bf16[16,16,128]{2,1,0:T(8,128)(2,1)S(1)} custom-call(bf16[16,16,128]{2,1,0:T(8,128)(2,1)} %q_hbm.1, bf16[16,2,256,128]{3,2,1,0:T(8,128)(2,1)} %k_hbm.1, bf16[16,2,256,128]{3,2,1,0:T(8,128)(2,1)} %v_hbm.1, f32[2,16,16]{2,1,0:T(8,128)} %gate_hbm.1, s32[16]{0:T(128)} %length_hbm.1, s32[16,2,16]{2,1,0:T(2,128)} %chosen_hbm.1, s32[2,16]{1,0:T(2,128)} %bitcast.1), custom_call_target="tpu_custom_call" | custom-call | tf_op jit(solution)/shard_map/decode/pallas_call | solution.py:344
  63.8 0.6 copy.9

commit v5 on v4

--- a/solution.py
+++ b/solution.py
@@ -123,11 +123,11 @@
     ]
     small[0].start()
     for c in range(LOADS):
-        load(0, c).start()
-    for copy in small[1:]:
-        copy.start()
-    for c in range(LOADS):
-        load(1, c).start()
+        for which in range(2):
+            load(which, c).start()
+        if c == 0:
+            for copy in small[1:]:
+                copy.start()
 
     root = ROOT
     away = lax.rem(root - me + n, n)
@@ -222,13 +222,14 @@
 
     per_load = rows // LOADS // CHUNK
     small[0].wait()
-    for which, chunk in ((0, score_chunk), (1, value_chunk)):
-        if which:
+    for c in range(LOADS):
+        load(0, c).wait()
+        lax.fori_loop(c * per_load, (c + 1) * per_load, score_chunk, 0)
+        if c == 0:
             for copy in small[1:]:
                 copy.wait()
-        for c in range(LOADS):
-            load(which, c).wait()
-            lax.fori_loop(c * per_load, (c + 1) * per_load, chunk, 0)
+        load(1, c).wait()
+        lax.fori_loop(c * per_load, (c + 1) * per_load, value_chunk, 0)
 
     pl.semaphore_wait(barrier, 2 * half + outside.astype(jnp.int32))
     offsets = sorted((d for d in range(1 - half, half + 1) if d != 0), key=lambda d: -abs(d))
@@ -266,7 +267,7 @@
         steps += [-(split + 1) * STRIDE] if k == split else []
         steps += [-STRIDE] if up + 1 < k else []
         copies = []
-        for i, step in enumerate(([-1] if k else []) + steps + [1, 2]):
+        for i, step in enumerate([-1] + steps + [1, 2] if k else [1] + steps):
             target = (ROOT + k * STRIDE + step) % n
             copies.append(remote(out_ref, out_ref, c_send.at[i], c_recv, target))
             copies[-1].start()
@@ -279,6 +280,13 @@
         block.start()
         block.wait_send()
         remote(out_ref, out_ref, c_send.at[0], c_recv, root).wait_recv()
+        second = remote(out_ref, out_ref, c_send.at[0], c_recv, (ROOT + 2) % n)
+
+        @pl.when(me == (ROOT + 1) % n)
+        def _():
+            second.start()
+            second.wait_send()
+
         for k in range(1, relays):
 
             @pl.when(me == (ROOT + k * STRIDE) % n)

time: 64.6 us -> 64.5 us (level)
  no operation moved by 1% of the time
where the time goes in v5:
time: 64.5 us; the launch traced here: 64.3 us
  Pallas kernels  63.7 us (99%)
    pallas_call x1, Pallas kernels, on_device(): pl.pallas_call(functools.partial(kernel, n), name='decode', out_shape=plt...  63.7 us

profile of v5, /device:TPU:40, one launch (start us, length us, event | category | flops | bytes accessed | tf_op | source)
XLA Modules:
  0.0 64.3 jit_solution(7755656757600962540)
XLA Ops:
  0.0 63.7 %decode.1 = bf16[16,16,128]{2,1,0:T(8,128)(2,1)S(1)} custom-call(bf16[16,16,128]{2,1,0:T(8,128)(2,1)} %q_hbm.1, bf16[16,2,256,128]{3,2,1,0:T(8,128)(2,1)} %k_hbm.1, bf16[16,2,256,128]{3,2,1,0:T(8,128)(2,1)} %v_hbm.1, f32[2,16,16]{2,1,0:T(8,128)} %gate_hbm.1, s32[16]{0:T(128)} %length_hbm.1, s32[16,2,16]{2,1,0:T(2,128)} %chosen_hbm.1, s32[2,16]{1,0:T(2,128)} %bitcast.1), custom_call_target="tpu_custom_call" | custom-call | tf_op jit(solution)/shard_map/decode/pallas_call | solution.py:352
  63.7 0.6 copy.9
